TPU v7x, 32 devices: a whole 2x2x4 slice. The times are simulated.
32 devices in a mesh: rep: 4 (over y, x), fsdp: 8 (over z, core).
Axes of the slice: x: 2, y: 2, z: 4, core: 2. Of those that a mesh axis runs over, the one named last changes fastest.
Arguments:
- inputs: bfloat16 [32, 1024, 768], P(('rep', 'fsdp')), may hold values from -6 to 6
- w_query: bfloat16 [768, 768], P('fsdp'), may hold values from -0.21875 to 0.21875
- w_key: bfloat16 [768, 768], P('fsdp'), may hold values from -0.21875 to 0.21875
- w_value: bfloat16 [768, 768], P('fsdp'), may hold values from -0.21875 to 0.21875
- w_out: bfloat16 [768, 768], P('fsdp'), may hold values from -0.875 to 0.875
- w_gate: bfloat16 [768, 2048], P('fsdp'), may hold values from -0.21875 to 0.21875
- w_up: bfloat16 [768, 2048], P('fsdp'), may hold values from -0.21875 to 0.21875
- w_down: bfloat16 [2048, 768], P('fsdp'), may hold values from -0.125 to 0.125
- norm_attn: bfloat16 [768], P('fsdp'), may hold values from 0.25 to 1.75
- norm_ffn: bfloat16 [768], P('fsdp'), may hold values from 0.25 to 1.75
- lengths: int32 [32], P(('rep', 'fsdp')), may hold values from 64 to 1024, as said below
- cotangent: bfloat16 [32, 1024, 768], P(('rep', 'fsdp')), may hold values from -6 to 6
Outputs:
- output: bfloat16 [32, 1024, 768], P(('rep', 'fsdp'))
- grad_input: bfloat16 [32, 1024, 768], P(('rep', 'fsdp'))
- grad_query: float32 [768, 768], P('fsdp')
- grad_key: float32 [768, 768], P('fsdp')
- grad_value: float32 [768, 768], P('fsdp')
- grad_out: float32 [768, 768], P('fsdp')
- grad_gate: float32 [768, 2048], P('fsdp')
- grad_up: float32 [768, 2048], P('fsdp')
- grad_down: float32 [2048, 768], P('fsdp')
- grad_norm_attn: float32 [768], P('fsdp')
- grad_norm_ffn: float32 [768], P('fsdp')
Inputs may be any that keep to these rules, and one draw needn't show every extreme that they name: Tokens at positions lengths[s] and beyond are padding. Some sequence has exactly 1024 valid tokens.
All inputs are finite; a program needn't handle non-finite values.
Results may differ from a plain program's by a relative error of at most 0.018.
Values may be sent and summed in bfloat16 or wider, within the bound.
No kernel may reach another device: no remote copies, remote signals or barrier semaphores. Data moves between devices by JAX's collectives and lax.ppermute only.
A program may use at most 192 MiB of HBM per device.

v0:
```python
import jax
import jax.numpy as jnp
from jax import lax
from jax.sharding import PartitionSpec as P

HEADS = 12
EPSILON = 1e-05


def rotary_tables(seq_length, head_width):
    half_width = head_width // 2
    position = jnp.arange(seq_length, dtype=jnp.float32)
    inverse = 10000.0 ** (-(jnp.arange(half_width, dtype=jnp.float32) * 2.0 / head_width))
    angles = position[:, None] * inverse[None, :]
    return (jnp.cos(angles)[:, None, :], jnp.sin(angles)[:, None, :])


def rotate(values, cosine, sine_table):
    half_width = values.shape[-1] // 2
    former = values[..., :half_width]
    latter = values[..., half_width:]
    return jnp.concatenate(
        [former * cosine - latter * sine_table, latter * cosine + former * sine_table], axis=-1
    )


def unrotate(grads_in, cosine, sine_table):
    half_width = grads_in.shape[-1] // 2
    former = grads_in[..., :half_width]
    latter = grads_in[..., half_width:]
    return jnp.concatenate(
        [former * cosine + latter * sine_table, latter * cosine - former * sine_table], axis=-1
    )


def rms_parts(values):
    inv_rms = lax.rsqrt(jnp.mean(values * values, axis=-1, keepdims=True) + EPSILON)
    return (values * inv_rms, inv_rms)


def norm_back(grad_normed, normed, inv_rms, gain):
    grad_gain = jnp.sum(grad_normed * normed, axis=0)
    scaled = grad_normed * gain
    return (
        inv_rms * (scaled - normed * jnp.mean(scaled * normed, axis=-1, keepdims=True)),
        grad_gain,
    )


def local(
    inputs,
    w_query,
    w_key,
    w_value,
    w_out,
    w_gate,
    w_up,
    w_down,
    norm_attn,
    norm_ffn,
    lengths,
    cotangent,
):
    gathered = (
        lax.all_gather(w_query, "fsdp", axis=0, tiled=True),
        lax.all_gather(w_key, "fsdp", axis=0, tiled=True),
        lax.all_gather(w_value, "fsdp", axis=0, tiled=True),
        lax.all_gather(w_out, "fsdp", axis=0, tiled=True),
        lax.all_gather(w_gate, "fsdp", axis=0, tiled=True),
        lax.all_gather(w_up, "fsdp", axis=0, tiled=True),
        lax.all_gather(w_down, "fsdp", axis=0, tiled=True),
        lax.all_gather(norm_attn, "fsdp", axis=0, tiled=True),
        lax.all_gather(norm_ffn, "fsdp", axis=0, tiled=True),
    )
    seq_count, seq_length, model_width = inputs.shape
    head_count = HEADS
    head_width = model_width // head_count
    row_count = seq_count * seq_length
    score_scale = head_width ** (-0.5)
    cosine, sine_table = rotary_tables(seq_length, head_width)
    position = jnp.arange(seq_length, dtype=jnp.int32)
    allowed = (position[None, None, :] <= position[None, :, None]) & (
        position[None, None, :] < lengths[:, None, None]
    )
    shape_heads = (seq_count, seq_length, head_count, head_width)

    def split_heads(values):
        return values.reshape(shape_heads).transpose(2, 0, 1, 3)

    def join_heads(values):
        return values.transpose(1, 2, 0, 3)

    inputs_f = inputs.reshape(row_count, model_width).astype(jnp.float32)
    normed_one, inv_one = rms_parts(inputs_f)
    gain_attn = gathered[7].astype(jnp.float32)
    gain_ffn = gathered[8].astype(jnp.float32)
    h_attn = (normed_one * gain_attn).astype(jnp.bfloat16)
    query_raw = jnp.dot(h_attn, gathered[0], preferred_element_type=jnp.float32)
    key_raw = jnp.dot(h_attn, gathered[1], preferred_element_type=jnp.float32)
    query_heads = split_heads(
        rotate(query_raw.reshape(shape_heads), cosine, sine_table)
        .astype(jnp.bfloat16)
        .reshape(row_count, model_width)
    )
    key_heads = split_heads(
        rotate(key_raw.reshape(shape_heads), cosine, sine_table)
        .astype(jnp.bfloat16)
        .reshape(row_count, model_width)
    )
    value_heads = split_heads(
        jnp.dot(h_attn, gathered[2], preferred_element_type=jnp.float32).astype(jnp.bfloat16)
    )

    def head_forward(operands):
        query_head, key_head, value_head = operands
        scores = (
            jnp.einsum("sqe,ske->sqk", query_head, key_head, preferred_element_type=jnp.float32)
            * score_scale
        )
        scores = jnp.where(allowed, scores, -1e30)
        row_max = jnp.max(scores, axis=-1, keepdims=True)
        exponent = jnp.exp(scores - row_max)
        row_sum = jnp.sum(exponent, axis=-1, keepdims=True)
        attention = (exponent / row_sum).astype(jnp.bfloat16)
        mixed = jnp.einsum(
            "sqk,ske->sqe", attention, value_head, preferred_element_type=jnp.float32
        )
        return (mixed, (row_max + jnp.log(row_sum))[..., 0])

    mixed_heads, log_sums = lax.map(head_forward, (query_heads, key_heads, value_heads))
    mixed_rows = join_heads(mixed_heads.astype(jnp.bfloat16)).reshape(row_count, model_width)
    residual = inputs_f + jnp.dot(mixed_rows, gathered[3], preferred_element_type=jnp.float32)
    normed_two, inv_two = rms_parts(residual)
    h_ffn = (normed_two * gain_ffn).astype(jnp.bfloat16)
    gate_proj = jnp.dot(h_ffn, gathered[4], preferred_element_type=jnp.float32)
    up_proj = jnp.dot(h_ffn, gathered[5], preferred_element_type=jnp.float32)
    sigmoid_gate = jax.nn.sigmoid(gate_proj)
    silu_gate = gate_proj * sigmoid_gate
    hidden = (silu_gate * up_proj).astype(jnp.bfloat16)
    ffn_out = jnp.dot(hidden, gathered[6], preferred_element_type=jnp.float32)
    output = (residual + ffn_out).astype(jnp.bfloat16).reshape(seq_count, seq_length, model_width)
    weights_bk = (
        lax.all_gather(w_query, "fsdp", axis=0, tiled=True),
        lax.all_gather(w_key, "fsdp", axis=0, tiled=True),
        lax.all_gather(w_value, "fsdp", axis=0, tiled=True),
        lax.all_gather(w_out, "fsdp", axis=0, tiled=True),
        lax.all_gather(w_gate, "fsdp", axis=0, tiled=True),
        lax.all_gather(w_up, "fsdp", axis=0, tiled=True),
        lax.all_gather(w_down, "fsdp", axis=0, tiled=True),
        lax.all_gather(norm_attn, "fsdp", axis=0, tiled=True),
        lax.all_gather(norm_ffn, "fsdp", axis=0, tiled=True),
    )
    valid_rows = (position[None, :] < lengths[:, None]).astype(jnp.float32).reshape(row_count, 1)
    grad_output = cotangent.reshape(row_count, model_width).astype(jnp.float32) * valid_rows
    grad_out_b = grad_output.astype(jnp.bfloat16)
    grad_down = jnp.einsum("rf,rd->fd", hidden, grad_out_b, preferred_element_type=jnp.float32)
    grad_hidden = jnp.einsum(
        "rd,fd->rf", grad_out_b, weights_bk[6], preferred_element_type=jnp.float32
    )
    grad_gate_b = (
        grad_hidden * up_proj * sigmoid_gate * (1.0 + gate_proj * (1.0 - sigmoid_gate))
    ).astype(jnp.bfloat16)
    grad_up_b = (grad_hidden * silu_gate).astype(jnp.bfloat16)
    grad_gate = jnp.einsum("rd,rf->df", h_ffn, grad_gate_b, preferred_element_type=jnp.float32)
    grad_up = jnp.einsum("rd,rf->df", h_ffn, grad_up_b, preferred_element_type=jnp.float32)
    grad_h_ffn = jnp.einsum(
        "rf,df->rd", grad_gate_b, weights_bk[4], preferred_element_type=jnp.float32
    )
    grad_h_ffn = grad_h_ffn + jnp.einsum(
        "rf,df->rd", grad_up_b, weights_bk[5], preferred_element_type=jnp.float32
    )
    grad_res_norm, grad_norm_ffn = norm_back(
        grad_h_ffn, normed_two, inv_two, weights_bk[8].astype(jnp.float32)
    )
    grad_residual = grad_output + grad_res_norm
    grad_attn_b = grad_residual.astype(jnp.bfloat16)
    grad_out = jnp.einsum("rd,re->de", mixed_rows, grad_attn_b, preferred_element_type=jnp.float32)
    grad_mixed = jnp.einsum(
        "re,de->rd", grad_attn_b, weights_bk[3], preferred_element_type=jnp.float32
    ).astype(jnp.bfloat16)
    grad_mixed_heads = split_heads(grad_mixed)

    def head_backward(operands):
        query_head, key_head, value_head, grad_head, log_head = operands
        scores = (
            jnp.einsum("sqe,ske->sqk", query_head, key_head, preferred_element_type=jnp.float32)
            * score_scale
        )
        scores = jnp.where(allowed, scores, -1e30)
        attention = jnp.exp(scores - log_head[..., None])
        attention_b = attention.astype(jnp.bfloat16)
        grad_attention = jnp.einsum(
            "sqe,ske->sqk", grad_head, value_head, preferred_element_type=jnp.float32
        )
        grad_scores = (
            attention
            * (grad_attention - jnp.sum(attention * grad_attention, axis=-1, keepdims=True))
        ).astype(jnp.bfloat16)
        grad_query_head = (
            jnp.einsum("sqk,ske->sqe", grad_scores, key_head, preferred_element_type=jnp.float32)
            * score_scale
        )
        grad_key_head = (
            jnp.einsum("sqk,sqe->ske", grad_scores, query_head, preferred_element_type=jnp.float32)
            * score_scale
        )
        grad_value_head = jnp.einsum(
            "sqk,sqe->ske", attention_b, grad_head, preferred_element_type=jnp.float32
        )
        return (grad_query_head, grad_key_head, grad_value_head)

    grad_q_heads, grad_k_heads, grad_v_heads = lax.map(
        head_backward, (query_heads, key_heads, value_heads, grad_mixed_heads, log_sums)
    )
    grad_q_rows = (
        unrotate(join_heads(grad_q_heads), cosine, sine_table)
        .reshape(row_count, model_width)
        .astype(jnp.bfloat16)
    )
    grad_k_rows = (
        unrotate(join_heads(grad_k_heads), cosine, sine_table)
        .reshape(row_count, model_width)
        .astype(jnp.bfloat16)
    )
    grad_v_rows = join_heads(grad_v_heads).reshape(row_count, model_width).astype(jnp.bfloat16)
    grad_query = jnp.einsum("rd,re->de", h_attn, grad_q_rows, preferred_element_type=jnp.float32)
    grad_key = jnp.einsum("rd,re->de", h_attn, grad_k_rows, preferred_element_type=jnp.float32)
    grad_value = jnp.einsum("rd,re->de", h_attn, grad_v_rows, preferred_element_type=jnp.float32)
    grad_h_attn = jnp.einsum(
        "re,de->rd", grad_q_rows, weights_bk[0], preferred_element_type=jnp.float32
    )
    grad_h_attn = grad_h_attn + jnp.einsum(
        "re,de->rd", grad_k_rows, weights_bk[1], preferred_element_type=jnp.float32
    )
    grad_h_attn = grad_h_attn + jnp.einsum(
        "re,de->rd", grad_v_rows, weights_bk[2], preferred_element_type=jnp.float32
    )
    grad_in_norm, grad_norm_attn = norm_back(
        grad_h_attn, normed_one, inv_one, weights_bk[7].astype(jnp.float32)
    )
    grad_input = (
        (grad_residual + grad_in_norm)
        .astype(jnp.bfloat16)
        .reshape(seq_count, seq_length, model_width)
    )
    owned = (
        lax.psum_scatter(grad_query, "fsdp", scatter_dimension=0, tiled=True),
        lax.psum_scatter(grad_key, "fsdp", scatter_dimension=0, tiled=True),
        lax.psum_scatter(grad_value, "fsdp", scatter_dimension=0, tiled=True),
        lax.psum_scatter(grad_out, "fsdp", scatter_dimension=0, tiled=True),
        lax.psum_scatter(grad_gate, "fsdp", scatter_dimension=0, tiled=True),
        lax.psum_scatter(grad_up, "fsdp", scatter_dimension=0, tiled=True),
        lax.psum_scatter(grad_down, "fsdp", scatter_dimension=0, tiled=True),
        lax.psum_scatter(grad_norm_attn, "fsdp", scatter_dimension=0, tiled=True),
        lax.psum_scatter(grad_norm_ffn, "fsdp", scatter_dimension=0, tiled=True),
    )
    reduced = (
        lax.psum(owned[0].astype(jnp.bfloat16), "rep").astype(jnp.float32),
        lax.psum(owned[1].astype(jnp.bfloat16), "rep").astype(jnp.float32),
        lax.psum(owned[2].astype(jnp.bfloat16), "rep").astype(jnp.float32),
        lax.psum(owned[3].astype(jnp.bfloat16), "rep").astype(jnp.float32),
        lax.psum(owned[4].astype(jnp.bfloat16), "rep").astype(jnp.float32),
        lax.psum(owned[5].astype(jnp.bfloat16), "rep").astype(jnp.float32),
        lax.psum(owned[6].astype(jnp.bfloat16), "rep").astype(jnp.float32),
        lax.psum(owned[7].astype(jnp.bfloat16), "rep").astype(jnp.float32),
        lax.psum(owned[8].astype(jnp.bfloat16), "rep").astype(jnp.float32),
    )
    return (
        output,
        grad_input,
        reduced[0],
        reduced[1],
        reduced[2],
        reduced[3],
        reduced[4],
        reduced[5],
        reduced[6],
        reduced[7],
        reduced[8],
    )


def solution(mesh):
    return jax.shard_map(
        local,
        mesh=mesh,
        in_specs=(
            P(("rep", "fsdp"), None, None),
            P("fsdp", None),
            P("fsdp", None),
            P("fsdp", None),
            P("fsdp", None),
            P("fsdp", None),
            P("fsdp", None),
            P("fsdp", None),
            P("fsdp"),
            P("fsdp"),
            P(("rep", "fsdp")),
            P(("rep", "fsdp"), None, None),
        ),
        out_specs=(
            P(("rep", "fsdp"), None, None),
            P(("rep", "fsdp"), None, None),
            P("fsdp", None),
            P("fsdp", None),
            P("fsdp", None),
            P("fsdp", None),
            P("fsdp", None),
            P("fsdp", None),
            P("fsdp", None),
            P("fsdp"),
            P("fsdp"),
        ),
        check_vma=False,
    )
```

profile of v0, /device:TPU:0, one launch (start us, length us, event | category | flops | bytes accessed | tf_op | source)
XLA Modules:
  0.0 832.0 jit_solution(13768503767765881324)
XLA Ops:
  16.6 18.5 %all-reduce.5 = (bf16[768]{0:T(1024)(128)(2,1)S(1)}, bf16[768]{0:T(1024)(128)(2,1)S(1)}) all-reduce(bf16[768]{0:T(1024)(128)(2,1)S(1)} %dynamic-update-slice, bf16[768]{0:T(1024)(128)(2,1)S(1)} %dynamic-update-slice.1), channel_id=1, replica_groups=mesh['rep'=4,'fsdp'=8] {'fsdp'}, use_global_device_ids=true, to_apply=%add | all-reduce | flops 1536 | bytes 6144
  36.4 2.6 copy.54
  40.6 18.7 %all-gather.8.cloned.1.call-done = bf16[768,768]{1,0:T(8,128)(2,1)} async-done(((bf16[96,768]{1,0:T(8,128)(2,1)}), bf16[768,768]{1,0:T(8,128)(2,1)}) %all-gather.8.cloned.1.call-update) | async-done | bytes 1179664 | tf_op jit(solution)/shard_map/all_gather | solution.py:65
  67.3 4.1 copy.51
  71.5 2.7 copy.52
  74.2 9.2 %all-gather.12.cloned.1.call-done = bf16[768,768]{1,0:T(8,128)(2,1)} async-done(((bf16[96,768]{1,0:T(8,128)(2,1)}), bf16[768,768]{1,0:T(8,128)(2,1)}) %all-gather.12.cloned.1.call-update) | async-done | bytes 1179664 | tf_op jit(solution)/shard_map/all_gather | solution.py:67
  83.4 3.9 convolution_convert_fusion.1
  87.3 4.2 copy.50
  91.6 68.2 %while.30 = (s32[]{:T(128)}, bf16[12,1,1024,64]{2,3,1,0:T(8,128)(2,1)S(1)}, f32[12,1,1024]{2,1,0:T(1,128)S(1)}, bf16[12,1,1024,64]{3,2,1,0:T(8,128)(2,1)}, bf16[...) while((s32[]{:T(128)}, ...), condition=%wide.region_4.5_spmd.clone.clone, body=%wide.region_1.4_spmd.clone.sunk.clone | while | flops 287308800 | bytes 13677649 | solution.py:130
  159.8 2.9 multiply_reduce_fusion.3
  165.9 9.2 %fusion.106 = f32[1024,2048]{1,0:T(8,128)} fusion(bf16[1024,768]{0,1:T(8,128)(2,1)} %multiply_convert_fusion.4, bf16[768,2048]{1,0:T(8,128)(2,1)} %all-gather.16.cloned.1.call-done), kind=kOutput, calls=%fused_computation.144 | convolution fusion | flops 3221225472 | bytes 13107200 | tf_op jit(solution)/shard_map/dot_general | solution.py:135
  175.0 10.3 %all-gather.18.cloned.1.call-done = bf16[768,2048]{1,0:T(8,128)(2,1)} async-done(((bf16[96,2048]{1,0:T(8,128)(2,1)}), bf16[768,2048]{1,0:T(8,128)(2,1)}) %all-gather.18.cloned.1.call-update) | async-done | bytes 3145744 | tf_op jit(solution)/shard_map/all_gather | solution.py:70
  185.4 9.2 %fusion.107 = f32[1024,2048]{1,0:T(8,128)} fusion(bf16[1024,768]{0,1:T(8,128)(2,1)} %multiply_convert_fusion.4, bf16[768,2048]{1,0:T(8,128)(2,1)} %all-gather.18.cloned.1.call-done), kind=kOutput, calls=%fused_computation.145 | convolution fusion | flops 3221225472 | bytes 13107200 | tf_op jit(solution)/shard_map/dot_general | solution.py:136
  194.6 29.6 %all-gather.20.cloned.1.call-done = bf16[2048,768]{1,0:T(8,128)(2,1)} async-done(((bf16[256,768]{1,0:T(8,128)(2,1)}), bf16[2048,768]{1,0:T(8,128)(2,1)}) %all-gather.20.cloned.1.call-update) | async-done | bytes 3145744 | tf_op jit(solution)/shard_map/all_gather | solution.py:71
  224.2 14.8 %multiply_convert_fusion.1 = (bf16[1024,2048]{1,0:T(8,128)(2,1)S(1)}, bf16[1024,2048]{1,0:T(8,128)(2,1)}, bf16[1024,2048]{1,0:T(8,128)(2,1)}) fusion(f32[1024,2048]{1,0:T(8,128)} %fusion.106, f32[1024,2048]{1,0:T(8,128)} %fusion.107, bf16[2048,768]{1,0:T(8,128)(2,1)} %all-gather.20.cloned.1.call-done, bf16[1,1024,768]{1,2,0:T(8,128)(2,1)} %copy.54, ...), kind=kOutput, calls=%fused_computation.63 | convolution fusion | flops 3255042048 | bytes 34082816 | tf_op jit(solution)/shard_map/rd,fd->rf/dot_general | solution.py:157
  239.0 7.4 fusion.108
  246.4 4.0 multiply_reduce_fusion.1
  253.0 2.9 fusion.93
  255.8 4.8 convolution_convert_fusion
  260.7 4.3 copy.57
  265.0 149.9 %while.31 = (s32[]{:T(128)}, f32[12,1,1024,64]{2,3,1,0:T(8,128)}, f32[12,1,1024,64]{2,3,1,0:T(8,128)}, bf16[12,1,1024,64]{2,3,1,0:T(8,128)(2,1)S(1)}, bf16[12,1,...) while((s32[]{:T(128)}, f32[12,1,1024,64]{2,3,1,0:T(8,128)}, ...), condition=%wide.region_9.10_spmd.clone.clone, body=%wide.region_7.9_spmd.clone.sunk.clone | while | flops 682753024 | bytes 34105448 | solution.py:212
  267.0 3.2 multiply_reduce_fusion.6
  271.3 2.5 fusion.193
  279.5 3.2 multiply_reduce_fusion.6
  283.8 2.4 fusion.193
  292.0 3.2 multiply_reduce_fusion.6
  296.3 2.4 fusion.193
  304.4 3.2 multiply_reduce_fusion.6
  316.9 3.2 multiply_reduce_fusion.6
  329.3 3.2 multiply_reduce_fusion.6
  333.7 2.4 fusion.193
  341.8 3.2 multiply_reduce_fusion.6
  346.2 2.4 fusion.193
  354.3 3.2 multiply_reduce_fusion.6
  358.6 2.4 fusion.193
  366.8 3.2 multiply_reduce_fusion.6
  371.1 2.4 fusion.193
  379.2 3.2 multiply_reduce_fusion.6
  391.7 3.2 multiply_reduce_fusion.6
  396.1 2.4 fusion.193
  404.2 3.2 multiply_reduce_fusion.6
  408.6 2.4 fusion.193
  414.9 5.0 multiply_add_fusion
  421.3 2.9 fusion.84
  426.8 2.9 fusion.80
  429.8 2.9 fusion.82
  432.8 8.7 %fusion.109 = f32[768,2048]{1,0:T(8,128)} fusion(bf16[1024,768]{0,1:T(8,128)(2,1)} %multiply_convert_fusion.4, bf16[1024,2048]{1,0:T(8,128)(2,1)} %get-tuple-element.260), kind=kOutput, calls=%fused_computation.147 | convolution fusion | flops 3221225472 | bytes 12058624 | tf_op jit(solution)/shard_map/rd,rf->df/dot_general | solution.py:164
  441.8 8.7 %fusion.110 = f32[768,2048]{1,0:T(8,128)} fusion(bf16[1024,768]{0,1:T(8,128)(2,1)} %multiply_convert_fusion.4, bf16[1024,2048]{1,0:T(8,128)(2,1)} %copy-done.30), kind=kOutput, calls=%fused_computation.148 | convolution fusion | flops 3221225472 | bytes 12058624 | tf_op jit(solution)/shard_map/rd,rf->df/dot_general | solution.py:165
  450.6 8.9 %fusion.89 = f32[2048,768]{1,0:T(8,128)} fusion(bf16[1024,2048]{1,0:T(8,128)(2,1)} %get-tuple-element.261, bf16[1,1024,768]{1,2,0:T(8,128)(2,1)} %copy.54, f32[1024]{0:T(1024)S(1)} %fusion.98), kind=kOutput, calls=%fused_computation.125 | convolution fusion | flops 3223584768 | bytes 12062720 | tf_op jit(solution)/shard_map/rf,rd->fd/dot_general | solution.py:156
  460.3 5.0 fusion.112
  465.3 3.0 fusion.111
  471.6 26.8 %reduce-scatter.8.cloned.1.call-done = f32[96,768]{1,0:T(8,128)} async-done(((f32[768,768]{1,0:T(8,128)}), f32[96,768]{1,0:T(8,128)}) %reduce-scatter.8.cloned.1.call-update) | async-done | bytes 294928 | tf_op jit(solution)/shard_map/reduce_scatter | solution.py:247
  500.0 36.7 %reduce-scatter.12.cloned.1.call-done = f32[96,768]{1,0:T(8,128)} async-done(((f32[768,768]{1,0:T(8,128)}), f32[96,768]{1,0:T(8,128)}) %reduce-scatter.12.cloned.1.call-update) | async-done | bytes 294928 | tf_op jit(solution)/shard_map/reduce_scatter | solution.py:249
  538.4 69.1 %reduce-scatter.16.cloned.1.call-done = f32[96,2048]{1,0:T(8,128)} async-done(((f32[768,2048]{1,0:T(8,128)}), f32[96,2048]{1,0:T(8,128)}) %reduce-scatter.16.cloned.1.call-update) | async-done | bytes 786448 | tf_op jit(solution)/shard_map/reduce_scatter | solution.py:251
  609.4 68.6 %reduce-scatter.18.cloned.1.call-done = f32[96,2048]{1,0:T(8,128)} async-done(((f32[768,2048]{1,0:T(8,128)}), f32[96,2048]{1,0:T(8,128)}) %reduce-scatter.18.cloned.1.call-update) | async-done | bytes 786448 | tf_op jit(solution)/shard_map/reduce_scatter | solution.py:252
  679.9 68.4 %reduce-scatter.20.cloned.1.call-done = f32[256,768]{1,0:T(8,128)} async-done(((f32[2048,768]{1,0:T(8,128)}), f32[256,768]{1,0:T(8,128)}) %reduce-scatter.20.cloned.1.call-update) | async-done | bytes 786448 | tf_op jit(solution)/shard_map/reduce_scatter | solution.py:253
  750.3 6.6 fusion.70
  756.9 13.9 %all-reduce.4 = (bf16[768]{0:T(1024)(128)(2,1)S(1)}, bf16[768]{0:T(1024)(128)(2,1)S(1)}) all-reduce(f32[768]{0:T(1024)S(1)} %get-tuple-element.206, f32[768]{0:T(1024)S(1)} %get-tuple-element.204), channel_id=9, replica_groups=mesh['rep'=4,'fsdp'=8] {'fsdp'}, use_global_device_ids=true, to_apply=%region_26.27.clone | all-reduce | flops 1536 | bytes 9216
  771.0 10.5 %all-reduce.6 = (bf16[96]{0:T(256)(128)(2,1)S(1)}, bf16[96]{0:T(256)(128)(2,1)S(1)}) all-reduce(bf16[96]{0:T(256)(128)(2,1)S(1)} %dynamic-slice.9, bf16[96]{0:T(256)(128)(2,1)S(1)} %dynamic-slice.8), channel_id=1, replica_groups=mesh['rep'=4,'fsdp'=8] {'rep'}, use_global_device_ids=true, to_apply=%region_27.28 | all-reduce | flops 192 | bytes 768 | tf_op jit(solution)/shard_map/psum | solution.py:265
  782.5 4.8 fusion.76
  787.3 2.7 copy.66
  790.1 8.0 fusion.88
  798.1 2.6 copy.65
  800.7 15.6 %all-reduce.10.cloned.1.call-done = (bf16[96,768]{1,0:T(8,128)(2,1)}, bf16[96,768]{1,0:T(8,128)(2,1)}, bf16[96,768]{1,0:T(8,128)(2,1)}, bf16[96,768]{1,0:T(8,128...) async-done(((bf16[96,768]{1,0:T(8,128)(2,1)}, bf16[96,768]{1,0:T(8,128)(2,1)}, bf16[96,768]{1,0:T(8,128)(2,1)}, ...) | async-done | bytes 1769488 | tf_op jit(solution)/shard_map/psum | solution.py:258
  (269 shorter events, 207.7 us)
Async XLA Ops:
  7.2 31.8 %all-gather.10.cloned.1.call-start = ((), (), s32[]{:S(2)}) async-start(), calls=%async_computation.8 | async-start | bytes 1327104 | tf_op jit(solution)/shard_map/all_gather | solution.py:66
  7.9 51.4 %all-gather.8.cloned.1.call-start = ((), (), s32[]{:S(2)}) async-start(), calls=%async_computation.7 | async-start | bytes 1327104 | tf_op jit(solution)/shard_map/all_gather | solution.py:65
  8.7 74.7 %all-gather.12.cloned.1.call-start = ((), (), s32[]{:S(2)}) async-start(), calls=%async_computation.9 | async-start | bytes 1327104 | tf_op jit(solution)/shard_map/all_gather | solution.py:67
  9.4 150.4 %all-gather.14.cloned.1.call-start = ((), (), s32[]{:S(2)}) async-start(), calls=%async_computation.10 | async-start | bytes 1327104 | tf_op jit(solution)/shard_map/all_gather | solution.py:68
  10.0 155.9 %all-gather.16.cloned.1.call-start = ((), (), s32[]{:S(2)}) async-start(), calls=%async_computation.11 | async-start | bytes 3538944 | tf_op jit(solution)/shard_map/all_gather | solution.py:69
  10.6 174.8 %all-gather.18.cloned.1.call-start = ((), (), s32[]{:S(2)}) async-start(), calls=%async_computation.12 | async-start | bytes 3538944 | tf_op jit(solution)/shard_map/all_gather | solution.py:70
  11.1 213.0 %all-gather.20.cloned.1.call-start = ((), (), s32[]{:S(2)}) async-start(), calls=%async_computation.13 | async-start | bytes 3538944 | tf_op jit(solution)/shard_map/all_gather | solution.py:71
  11.9 456.4 %reduce-scatter.14.cloned.1.call-start = ((), (), s32[]{:S(2)}) async-start(), calls=%async_computation.17 | async-start | bytes 2654208 | tf_op jit(solution)/shard_map/reduce_scatter | solution.py:250
  12.0 2.9 copy-start.25
  12.0 4.2 copy-start.28
  12.0 4.4 copy-start.29
  12.2 24.2 %copy-start = (bf16[12,1,1024,64]{2,3,1,0:T(8,128)(2,1)}, bf16[12,1,1024,64]{2,3,1,0:T(8,128)(2,1)S(1)}, u32[]{:S(2)}) copy-start(bf16[12,1,1024,64]{2,3,1,0:T(8,128)(2,1)S(1)} %fusion.104) | copy-start | bytes 4718596
  14.9 68.5 %copy-start.21 = (f32[1024]{0:T(1024)}, f32[1024]{0:T(1024)S(1)}, u32[]{:S(2)}) copy-start(f32[1024]{0:T(1024)S(1)} %add_rsqrt_fusion.1) | copy-start | bytes 12292
  35.1 48.3 %copy-start.23 = (f32[768]{0:T(1024)}, f32[768]{0:T(1024)S(1)}, u32[]{:S(2)}) copy-start(f32[768]{0:T(1024)S(1)} %convert_element_type.215) | copy-start | bytes 9220
  35.6 29.1 %copy-start.11 = (f32[1024,32]{0,1:T(8,128)}, f32[1024,32]{0,1:T(8,128)S(1)}, u32[]{:S(2)}) copy-start(f32[1024,32]{0,1:T(8,128)S(1)} %get-tuple-element.278) | copy-start | bytes 393220
  35.7 29.1 %copy-start.13 = (f32[1024,32]{0,1:T(8,128)}, f32[1024,32]{0,1:T(8,128)S(1)}, u32[]{:S(2)}) copy-start(f32[1024,32]{0,1:T(8,128)S(1)} %get-tuple-element.279) | copy-start | bytes 393220
  61.7 1.5 copy-start.16
  87.3 4.2 copy-start.2
  162.8 1.6 copy-start.4
  224.2 14.8 %copy-start.26 = (bf16[768,2048]{1,0:T(8,128)(2,1)S(1)}, bf16[768,2048]{1,0:T(8,128)(2,1)}, u32[]{:S(2)}) copy-start(bf16[768,2048]{1,0:T(8,128)(2,1)} %all-gather.16.cloned.1.call-done) | copy-start | bytes 9437188
  239.0 7.4 copy-start.30
  239.0 7.4 copy-start.5
  239.0 7.4 copy-start.27
  246.4 4.0 copy-start.7
  251.3 1.7 copy-start.3
  260.7 4.3 copy-start.1
  264.9 205.0 %reduce-scatter.10.cloned.1.call-start = ((), (), s32[]{:S(2)}) async-start(), calls=%async_computation.15 | async-start | bytes 2654208 | tf_op jit(solution)/shard_map/reduce_scatter | solution.py:248
  265.0 149.9 %copy-start.12 = (f32[1024,32]{0,1:T(8,128)S(1)}, f32[1024,32]{0,1:T(8,128)}, u32[]{:S(2)}) copy-start(f32[1024,32]{0,1:T(8,128)} %copy-done.11) | copy-start | bytes 393220
  265.0 149.9 %copy-start.14 = (f32[1024,32]{0,1:T(8,128)S(1)}, f32[1024,32]{0,1:T(8,128)}, u32[]{:S(2)}) copy-start(f32[1024,32]{0,1:T(8,128)} %copy-done.13) | copy-start | bytes 393220
  419.9 1.3 copy-start.22
  419.9 1.3 copy-start.24
  420.1 1.2 copy-start.8
  424.1 74.3 %reduce-scatter.8.cloned.1.call-start = ((), (), s32[]{:S(2)}) async-start(), calls=%async_computation.14 | async-start | bytes 2654208 | tf_op jit(solution)/shard_map/reduce_scatter | solution.py:247
  425.7 1.1 copy-start.9
  429.7 107.0 %reduce-scatter.12.cloned.1.call-start = ((), (), s32[]{:S(2)}) async-start(), calls=%async_computation.16 | async-start | bytes 2654208 | tf_op jit(solution)/shard_map/reduce_scatter | solution.py:249
  432.7 174.8 %reduce-scatter.16.cloned.1.call-start = ((), (), s32[]{:S(2)}) async-start(), calls=%async_computation.18 | async-start | bytes 7077888 | tf_op jit(solution)/shard_map/reduce_scatter | solution.py:251
  441.5 236.5 %reduce-scatter.18.cloned.1.call-start = ((), (), s32[]{:S(2)}) async-start(), calls=%async_computation.19 | async-start | bytes 7077888 | tf_op jit(solution)/shard_map/reduce_scatter | solution.py:252
  450.6 297.8 %reduce-scatter.20.cloned.1.call-start = ((), (), s32[]{:S(2)}) async-start(), calls=%async_computation.20 | async-start | bytes 7077888 | tf_op jit(solution)/shard_map/reduce_scatter | solution.py:253
  459.5 356.7 %all-reduce.10.cloned.1.call-start = ((), (), s32[]{:S(2)}) async-start(), calls=%async_computation.21 | async-start | bytes 3538944 | tf_op jit(solution)/shard_map/psum | solution.py:258
  460.2 5.1 copy-start.10
  460.3 5.0 copy-start.15
  787.3 2.7 copy-start.6
  816.2 5.9 copy-start.20
  816.2 6.6 copy-start.19
  816.2 7.4 copy-start.18
  816.2 8.1 copy-start.17
Sparse Core Ops, SparseCore 0:
  9.6 25.6 all-gather.9
  37.0 22.2 all-gather.7
  60.9 22.4 all-gather.11
  84.9 22.4 all-gather.13
  108.8 37.8 all-gather.15
  148.2 37.1 all-gather.17
  187.0 37.1 all-gather.19
  265.1 35.9 reduce-scatter.13
  424.2 35.9 reduce-scatter.9
  462.4 35.9 reduce-scatter.7
  500.7 35.9 reduce-scatter.11
  538.9 68.5 reduce-scatter.15
  609.8 68.1 reduce-scatter.17
  680.2 68.1 reduce-scatter.19
  753.3 62.8 all-reduce.9
where the time goes:
time: 844 us; the launch traced here: 832 us
  waiting for transfers between devices  358 us (42%)
  matrix products  299 us (35%)
  other arithmetic  76.5 us (9%)
  blocking collectives  42.9 us (5%)
  local copies, waits for them, and re-layouts  36.6 us (4%)
  between operations  16.9 us (2%)
    reduce_scatter x1, waiting for transfers between devices, local(): lax.psum_scatter(grad_gate, 'fsdp', scatter_dimension=0, tiled=True)  69.1 us
    reduce_scatter x1, waiting for transfers between devices, local(): lax.psum_scatter(grad_up, 'fsdp', scatter_dimension=0, tiled=True)  68.6 us
    reduce_scatter x1, waiting for transfers between devices, local(): lax.psum_scatter(grad_down, 'fsdp', scatter_dimension=0, tiled=True)  68.4 us
    dot_general x12, matrix products, head_backward(): jnp.einsum('sqe,ske->sqk', query_head, key_head, preferred_element_type=j...  38.4 us
    reduce_scatter x1, waiting for transfers between devices, local(): lax.psum_scatter(grad_value, 'fsdp', scatter_dimension=0, tiled=True)  36.7 us
    unnamed x2, blocking collectives  32.4 us
    all_gather x1, waiting for transfers between devices, local(): lax.all_gather(w_down, 'fsdp', axis=0, tiled=True)  29.6 us
    dot_general x12, matrix products, head_backward(): jnp.einsum('sqk,sqe->ske', grad_scores, query_head, preferred_element_typ...  29.3 us
  transfers between devices with their start and end apart: 15, of which 10 were waited for; matrix products, arithmetic and copies ran while one was open for 43% of the time, Pallas kernels for 0%

commit v1 on v0

--- a/solution.py
+++ b/solution.py
@@ -5,6 +5,18 @@
 
 HEADS = 12
 EPSILON = 1e-05
+
+
+def gather_by_bits(value, axis, dim):
+    ways, here = (lax.axis_size(axis), lax.axis_index(axis))
+    grown, reach = (value, 1)
+    while reach < ways:
+        theirs = lax.ppermute(grown, axis, [(d, d ^ reach) for d in range(ways)])
+        mine_first = jnp.concatenate([grown, theirs], axis=dim)
+        theirs_first = jnp.concatenate([theirs, grown], axis=dim)
+        grown = jnp.where(here & reach == 0, mine_first, theirs_first)
+        reach = 2 * reach
+    return grown
 
 
 def rotary_tables(seq_length, head_width):
@@ -62,7 +74,7 @@
     cotangent,
 ):
     gathered = (
-        lax.all_gather(w_query, "fsdp", axis=0, tiled=True),
+        gather_by_bits(w_query, "fsdp", 0),
         lax.all_gather(w_key, "fsdp", axis=0, tiled=True),
         lax.all_gather(w_value, "fsdp", axis=0, tiled=True),
         lax.all_gather(w_out, "fsdp", axis=0, tiled=True),

time: 844 us -> 819 us (0.970)
  waiting for transfers between devices: 358 us -> 329 us
    ppermute x0 -> x3, waiting for transfers between devices: none -> 20.8 us  [gather_by_bits(): theirs = lax.ppermute(grown, axis, [(d, d ^ reach) for d in range(ways)])]
    all_gather x1, waiting for transfers between devices: 18.7 us -> 0.01 us  [local(): lax.all_gather(w_query, 'fsdp', axis=0, tiled=True)]
    all_gather x1, waiting for transfers between devices: 29.6 us -> 17.8 us  [local(): lax.all_gather(w_down, 'fsdp', axis=0, tiled=True)]
    all_gather x1, waiting for transfers between devices: 10.3 us -> 0.01 us  [local(): lax.all_gather(w_up, 'fsdp', axis=0, tiled=True)]
    all_gather x1, waiting for transfers between devices: 9.23 us -> 0.01 us  [local(): lax.all_gather(w_value, 'fsdp', axis=0, tiled=True)]
    unnamed x75 -> x78, local copies, waits for them, and re-layouts: 23.9 us -> 21.7 us
  transfers between devices with their start and end apart: 15 -> 18, of which waited for: 10 -> 9; matrix products, arithmetic and copies ran while one was open for 43% -> 48% of each run, Pallas kernels for 0% -> 0%
where the time goes in v1:
time: 819 us; the launch traced here: 813 us
  waiting for transfers between devices  329 us (40%)
  matrix products  299 us (37%)
  other arithmetic  78 us (10%)
  blocking collectives  49.6 us (6%)
  local copies, waits for them, and re-layouts  30.5 us (4%)
  between operations  16.7 us (2%)
  starting transfers between devices  8.65 us (1%)
    reduce_scatter x1, waiting for transfers between devices, local(): lax.psum_scatter(grad_gate, 'fsdp', scatter_dimension=0, tiled=True)  69.2 us
    reduce_scatter x1, waiting for transfers between devices, local(): lax.psum_scatter(grad_up, 'fsdp', scatter_dimension=0, tiled=True)  68.6 us
    reduce_scatter x1, waiting for transfers between devices, local(): lax.psum_scatter(grad_down, 'fsdp', scatter_dimension=0, tiled=True)  68.5 us
    unnamed x2, blocking collectives  39 us
    dot_general x12, matrix products, head_backward(): jnp.einsum('sqe,ske->sqk', query_head, key_head, preferred_element_type=j...  38.4 us
    reduce_scatter x1, waiting for transfers between devices, local(): lax.psum_scatter(grad_value, 'fsdp', scatter_dimension=0, tiled=True)  36.6 us
    dot_general x12, matrix products, head_backward(): jnp.einsum('sqk,sqe->ske', grad_scores, query_head, preferred_element_typ...  29.2 us
    dot_general x12, matrix products, head_backward(): jnp.einsum('sqk,ske->sqe', grad_scores, key_head, preferred_element_type=...  26.3 us
  transfers between devices with their start and end apart: 18, of which 9 were waited for; matrix products, arithmetic and copies ran while one was open for 48% of the time, Pallas kernels for 0%

profile of v1, /device:TPU:0, one launch (start us, length us, event | category | flops | bytes accessed | tf_op | source)
XLA Modules:
  0.0 813.0 jit_solution(10860290471594164008)
XLA Ops:
  15.0 2.6 collective-permute-start.1
  18.0 15.9 %collective-permute-done.1 = bf16[192,768]{0,1:T(8,128)(2,1)S(1)} collective-permute-done((bf16[192,768]{0,1:T(8,128)(2,1)S(1)}, bf16[192,768]{0,1:T(8,128)(2,1)S(1)}, u32[]{:S(2)}, u32[]{:S(2)}) %collective-permute-start.1) | collective-permute-done | bytes 294944 | tf_op jit(solution)/shard_map/ppermute | solution.py:14
  35.2 4.6 collective-permute-start.2
  41.6 25.1 %all-reduce.5 = (bf16[768]{0:T(1024)(128)(2,1)S(1)}, bf16[768]{0:T(1024)(128)(2,1)S(1)}) all-reduce(bf16[768]{0:T(1024)(128)(2,1)S(1)} %dynamic-update-slice, bf16[768]{0:T(1024)(128)(2,1)S(1)} %dynamic-update-slice.1), channel_id=1, replica_groups=mesh['rep'=4,'fsdp'=8] {'fsdp'}, use_global_device_ids=true, to_apply=%add | all-reduce | flops 1536 | bytes 6144
  66.8 2.6 copy.80
  70.0 4.9 collective-permute-done.2
  76.9 3.1 convolution_bitcast_fusion.1
  86.1 4.1 copy.77
  90.2 2.7 copy.78
  92.9 3.9 convolution_convert_fusion.1
  96.8 4.2 copy.76
  101.1 68.3 %while.30 = (s32[]{:T(128)}, bf16[12,1,1024,64]{2,3,1,0:T(8,128)(2,1)S(1)}, f32[12,1,1024]{2,1,0:T(1,128)S(1)}, bf16[12,1,1024,64]{3,2,1,0:T(8,128)(2,1)}, bf16[...) while((s32[]{:T(128)}, ...), condition=%wide.region_4.5_spmd.clone.clone, body=%wide.region_1.4_spmd.clone.sunk.clone | while | flops 287308800 | bytes 13677649 | solution.py:142
  169.4 3.5 multiply_reduce_fusion.3
  176.0 7.6 fusion.106
  183.6 9.2 %fusion.107 = f32[1024,2048]{1,0:T(8,128)} fusion(bf16[1024,768]{0,1:T(8,128)(2,1)} %copy-done.12, bf16[768,2048]{1,0:T(8,128)(2,1)} %all-gather.16.cloned.1.call-done), kind=kOutput, calls=%fused_computation.148 | convolution fusion | flops 3221225472 | bytes 13107200 | tf_op jit(solution)/shard_map/dot_general | solution.py:148
  192.8 17.8 %all-gather.18.cloned.1.call-done = bf16[2048,768]{1,0:T(8,128)(2,1)} async-done(((bf16[256,768]{1,0:T(8,128)(2,1)}), bf16[2048,768]{1,0:T(8,128)(2,1)}) %all-gather.18.cloned.1.call-update) | async-done | bytes 3145744 | tf_op jit(solution)/shard_map/all_gather | solution.py:83
  210.6 13.2 %multiply_convert_fusion.1 = (bf16[1024,2048]{1,0:T(8,128)(2,1)S(1)}, bf16[1024,2048]{1,0:T(8,128)(2,1)}, bf16[1024,2048]{1,0:T(8,128)(2,1)}) fusion(f32[1024,2048]{1,0:T(8,128)} %fusion.106, f32[1024,2048]{1,0:T(8,128)} %fusion.107, bf16[2048,768]{1,0:T(8,128)(2,1)} %all-gather.18.cloned.1.call-done, bf16[1,1024,768]{1,2,0:T(8,128)(2,1)S(1)} %copy-done.7, ...), kind=kOutput, calls=%fused_computation.63 | convolution fusion | flops 3255042048 | bytes 34082816 | tf_op jit(solution)/shard_map/rd,fd->rf/dot_general | solution.py:169
  223.9 7.2 fusion.108
  231.1 4.0 multiply_reduce_fusion.1
  238.0 2.7 copy.83
  240.8 5.4 fusion.93
  246.2 149.8 %while.31 = (s32[]{:T(128)}, f32[12,1,1024,64]{2,3,1,0:T(8,128)}, f32[12,1,1024,64]{2,3,1,0:T(8,128)}, bf16[12,1,1024,64]{2,3,1,0:T(8,128)(2,1)S(1)}, bf16[12,1,...) while((s32[]{:T(128)}, f32[12,1,1024,64]{2,3,1,0:T(8,128)}, ...), condition=%wide.region_9.10_spmd.clone.clone, body=%wide.region_7.9_spmd.clone.sunk.clone | while | flops 682753024 | bytes 34105448 | solution.py:224
  248.2 3.2 multiply_reduce_fusion.6
  252.5 2.4 fusion.193
  260.7 3.2 multiply_reduce_fusion.6
  265.0 2.4 fusion.193
  273.1 3.2 multiply_reduce_fusion.6
  285.6 3.2 multiply_reduce_fusion.6
  290.0 2.4 fusion.193
  298.1 3.2 multiply_reduce_fusion.6
  302.4 2.4 fusion.193
  310.5 3.2 multiply_reduce_fusion.6
  314.9 2.4 fusion.193
  323.0 3.2 multiply_reduce_fusion.6
  327.4 2.4 fusion.193
  335.5 3.2 multiply_reduce_fusion.6
  339.8 2.4 fusion.193
  347.9 3.2 multiply_reduce_fusion.6
  352.3 2.4 fusion.193
  360.4 3.2 multiply_reduce_fusion.6
  372.8 3.2 multiply_reduce_fusion.6
  377.2 2.4 fusion.193
  385.3 3.2 multiply_reduce_fusion.6
  389.7 2.4 fusion.193
  396.1 5.0 multiply_add_fusion
  402.4 2.9 fusion.84
  408.0 2.9 fusion.80
  411.0 2.9 fusion.82
  413.9 8.7 %fusion.109 = f32[768,2048]{1,0:T(8,128)} fusion(bf16[1024,768]{0,1:T(8,128)(2,1)} %copy-done.12, bf16[1024,2048]{1,0:T(8,128)(2,1)} %get-tuple-element.288), kind=kOutput, calls=%fused_computation.150 | convolution fusion | flops 3221225472 | bytes 12058624 | tf_op jit(solution)/shard_map/rd,rf->df/dot_general | solution.py:176
  423.0 8.7 %fusion.110 = f32[768,2048]{1,0:T(8,128)} fusion(bf16[1024,768]{0,1:T(8,128)(2,1)} %copy-done.12, bf16[1024,2048]{1,0:T(8,128)(2,1)} %copy-done.31), kind=kOutput, calls=%fused_computation.151 | convolution fusion | flops 3221225472 | bytes 12058624 | tf_op jit(solution)/shard_map/rd,rf->df/dot_general | solution.py:177
  431.8 8.9 %fusion.89 = f32[2048,768]{1,0:T(8,128)} fusion(bf16[1024,2048]{1,0:T(8,128)(2,1)} %get-tuple-element.289, bf16[1,1024,768]{1,2,0:T(8,128)(2,1)} %copy.80, f32[1024]{0:T(1024)S(1)} %fusion.98), kind=kOutput, calls=%fused_computation.125 | convolution fusion | flops 3223584768 | bytes 12062720 | tf_op jit(solution)/shard_map/rf,rd->fd/dot_general | solution.py:168
  441.4 4.9 fusion.112
  446.3 4.8 fusion.111
  454.3 25.2 %reduce-scatter.8.cloned.1.call-done = f32[96,768]{1,0:T(8,128)} async-done(((f32[768,768]{1,0:T(8,128)}), f32[96,768]{1,0:T(8,128)}) %reduce-scatter.8.cloned.1.call-update) | async-done | bytes 294928 | tf_op jit(solution)/shard_map/reduce_scatter | solution.py:259
  481.1 36.6 %reduce-scatter.12.cloned.1.call-done = f32[96,768]{1,0:T(8,128)} async-done(((f32[768,768]{1,0:T(8,128)}), f32[96,768]{1,0:T(8,128)}) %reduce-scatter.12.cloned.1.call-update) | async-done | bytes 294928 | tf_op jit(solution)/shard_map/reduce_scatter | solution.py:261
  519.4 69.2 %reduce-scatter.16.cloned.1.call-done = f32[96,2048]{1,0:T(8,128)} async-done(((f32[768,2048]{1,0:T(8,128)}), f32[96,2048]{1,0:T(8,128)}) %reduce-scatter.16.cloned.1.call-update) | async-done | bytes 786448 | tf_op jit(solution)/shard_map/reduce_scatter | solution.py:263
  590.6 68.6 %reduce-scatter.18.cloned.1.call-done = f32[96,2048]{1,0:T(8,128)} async-done(((f32[768,2048]{1,0:T(8,128)}), f32[96,2048]{1,0:T(8,128)}) %reduce-scatter.18.cloned.1.call-update) | async-done | bytes 786448 | tf_op jit(solution)/shard_map/reduce_scatter | solution.py:264
  661.1 68.5 %reduce-scatter.20.cloned.1.call-done = f32[256,768]{1,0:T(8,128)} async-done(((f32[2048,768]{1,0:T(8,128)}), f32[256,768]{1,0:T(8,128)}) %reduce-scatter.20.cloned.1.call-update) | async-done | bytes 786448 | tf_op jit(solution)/shard_map/reduce_scatter | solution.py:265
  731.5 6.6 fusion.70
  738.0 13.9 %all-reduce.4 = (bf16[768]{0:T(1024)(128)(2,1)S(1)}, bf16[768]{0:T(1024)(128)(2,1)S(1)}) all-reduce(f32[768]{0:T(1024)S(1)} %get-tuple-element.234, f32[768]{0:T(1024)S(1)} %get-tuple-element.232), channel_id=9, replica_groups=mesh['rep'=4,'fsdp'=8] {'fsdp'}, use_global_device_ids=true, to_apply=%region_26.27.clone | all-reduce | flops 1536 | bytes 9216
  752.1 10.5 %all-reduce.6 = (bf16[96]{0:T(256)(128)(2,1)S(1)}, bf16[96]{0:T(256)(128)(2,1)S(1)}) all-reduce(bf16[96]{0:T(256)(128)(2,1)S(1)} %dynamic-slice.9, bf16[96]{0:T(256)(128)(2,1)S(1)} %dynamic-slice.8), channel_id=1, replica_groups=mesh['rep'=4,'fsdp'=8] {'rep'}, use_global_device_ids=true, to_apply=%region_27.28 | all-reduce | flops 192 | bytes 768 | tf_op jit(solution)/shard_map/psum | solution.py:277
  763.7 3.7 fusion.76
  768.9 7.9 fusion.88
  778.4 19.0 %all-reduce.10.cloned.1.call-done = (bf16[96,768]{1,0:T(8,128)(2,1)}, bf16[96,768]{1,0:T(8,128)(2,1)}, bf16[96,768]{1,0:T(8,128)(2,1)}, bf16[96,768]{1,0:T(8,128...) async-done(((bf16[96,768]{1,0:T(8,128)(2,1)}, bf16[96,768]{1,0:T(8,128)(2,1)}, bf16[96,768]{1,0:T(8,128)(2,1)}, ...) | async-done | bytes 1769488 | tf_op jit(solution)/shard_map/psum | solution.py:270
  (280 shorter events, 208.4 us)
Async XLA Ops:
  7.2 5.7 copy-start.9
  7.2 72.8 %all-gather.8.cloned.1.call-start = ((), (), s32[]{:S(2)}) async-start(), calls=%async_computation.7 | async-start | bytes 1327104 | tf_op jit(solution)/shard_map/all_gather | solution.py:78
  7.9 85.0 %all-gather.10.cloned.1.call-start = ((), (), s32[]{:S(2)}) async-start(), calls=%async_computation.8 | async-start | bytes 1327104 | tf_op jit(solution)/shard_map/all_gather | solution.py:79
  8.7 160.7 %all-gather.12.cloned.1.call-start = ((), (), s32[]{:S(2)}) async-start(), calls=%async_computation.9 | async-start | bytes 1327104 | tf_op jit(solution)/shard_map/all_gather | solution.py:80
  9.4 165.4 %all-gather.14.cloned.1.call-start = ((), (), s32[]{:S(2)}) async-start(), calls=%async_computation.10 | async-start | bytes 3538944 | tf_op jit(solution)/shard_map/all_gather | solution.py:81
  10.0 173.6 %all-gather.16.cloned.1.call-start = ((), (), s32[]{:S(2)}) async-start(), calls=%async_computation.11 | async-start | bytes 3538944 | tf_op jit(solution)/shard_map/all_gather | solution.py:82
  10.6 200.0 %all-gather.18.cloned.1.call-start = ((), (), s32[]{:S(2)}) async-start(), calls=%async_computation.12 | async-start | bytes 3538944 | tf_op jit(solution)/shard_map/all_gather | solution.py:83
  11.1 435.1 %all-gather.20.cloned.1.call-start = ((), (), s32[]{:S(2)}) async-start(), calls=%async_computation.13 | async-start | bytes 1327104 | tf_op jit(solution)/shard_map/all_gather | solution.py:155
  12.3 2.3 collective-permute-start
  12.9 438.2 %reduce-scatter.14.cloned.1.call-start = ((), (), s32[]{:S(2)}) async-start(), calls=%async_computation.17 | async-start | bytes 2654208 | tf_op jit(solution)/shard_map/reduce_scatter | solution.py:262
  13.7 26.2 %copy-start.25 = (u32[32]{0:T(128)S(1)}, u32[32]{0:T(128)}, u32[]{:S(2)}) copy-start(u32[32]{0:T(128)} %constant.80) | copy-start | bytes 388
  13.7 27.4 %copy-start.29 = (bf16[96]{0:T(256)(128)(2,1)S(1)}, bf16[96]{0:T(256)(128)(2,1)}, u32[]{:S(2)}) copy-start(bf16[96]{0:T(256)(128)(2,1)} %param.24) | copy-start | bytes 580
  13.7 27.7 %copy-start.30 = (bf16[96]{0:T(256)(128)(2,1)S(1)}, bf16[96]{0:T(256)(128)(2,1)}, u32[]{:S(2)}) copy-start(bf16[96]{0:T(256)(128)(2,1)} %param.25) | copy-start | bytes 580
  14.6 52.2 %copy-start = (bf16[12,1,1024,64]{2,3,1,0:T(8,128)(2,1)}, bf16[12,1,1024,64]{2,3,1,0:T(8,128)(2,1)S(1)}, u32[]{:S(2)}) copy-start(bf16[12,1,1024,64]{2,3,1,0:T(8,128)(2,1)S(1)} %fusion.104) | copy-start | bytes 4718596
  15.0 18.9 %collective-permute-start.1 = (bf16[192,768]{0,1:T(8,128)(2,1)S(1)}, bf16[192,768]{0,1:T(8,128)(2,1)S(1)}, u32[]{:S(2)}, u32[]{:S(2)}) collective-permute-start(bf16[192,768]{0,1:T(8,128)(2,1)S(1)} %maximum_select_fusion.2), channel_id=1, source_target_pairs={{0,2},{1,3},{2,0},{3,1},{4,6},{5,7},{6,4},{7,5},{8,10},{9,11},{10,... | collective-permute-start | bytes 884744 | tf_op jit(solution)/shard_map/ppermute | solution.py:14
  35.2 39.7 %collective-permute-start.2 = (bf16[384,768]{0,1:T(8,128)(2,1)}, bf16[384,768]{0,1:T(8,128)(2,1)}, u32[]{:S(2)}, u32[]{:S(2)}) collective-permute-start(bf16[384,768]{0,1:T(8,128)(2,1)} %maximum_select_fusion.1), channel_id=1, source_target_pairs={{0,4},{1,5},{2,6},{3,7},{4,0},{5,1},{6,2},{7,3},{8,12},{9,13},{10,... | collective-permute-start | bytes 1769480 | tf_op jit(solution)/shard_map/ppermute | solution.py:14
  66.7 26.2 %copy-start.21 = (f32[768]{0:T(1024)}, f32[768]{0:T(1024)S(1)}, u32[]{:S(2)}) copy-start(f32[768]{0:T(1024)S(1)} %convert_element_type.215) | copy-start | bytes 9220
  69.4 23.5 %copy-start.23 = (f32[1024]{0:T(1024)}, f32[1024]{0:T(1024)S(1)}, u32[]{:S(2)}) copy-start(f32[1024]{0:T(1024)S(1)} %add_rsqrt_fusion.1) | copy-start | bytes 12292
  69.9 13.2 %copy-start.13 = (f32[1024,32]{0,1:T(8,128)}, f32[1024,32]{0,1:T(8,128)S(1)}, u32[]{:S(2)}) copy-start(f32[1024,32]{0,1:T(8,128)S(1)} %get-tuple-element.306) | copy-start | bytes 393220
  69.9 13.2 %copy-start.15 = (f32[1024,32]{0,1:T(8,128)}, f32[1024,32]{0,1:T(8,128)S(1)}, u32[]{:S(2)}) copy-start(f32[1024,32]{0,1:T(8,128)S(1)} %get-tuple-element.307) | copy-start | bytes 393220
  81.6 1.9 copy-start.8
  96.8 4.2 copy-start.3
  169.3 3.5 copy-start.2
  172.9 1.6 copy-start.5
  174.8 1.1 copy-start.12
  183.6 27.1 %copy-start.7 = (bf16[1,1024,768]{1,2,0:T(8,128)(2,1)S(1)}, bf16[1,1024,768]{1,2,0:T(8,128)(2,1)}, u32[]{:S(2)}) copy-start(bf16[1,1024,768]{1,2,0:T(8,128)(2,1)} %copy.80) | copy-start | bytes 4718596
  210.6 13.2 %copy-start.26 = (bf16[768,2048]{1,0:T(8,128)(2,1)S(1)}, bf16[768,2048]{1,0:T(8,128)(2,1)}, u32[]{:S(2)}) copy-start(bf16[768,2048]{1,0:T(8,128)(2,1)} %all-gather.14.cloned.1.call-done) | copy-start | bytes 9437188
  223.8 7.3 copy-start.31
  223.8 7.3 copy-start.6
  223.8 7.3 copy-start.27
  235.1 1.3 copy-start.28
  236.4 1.7 copy-start.4
  240.8 5.5 copy-start.1
  246.2 206.5 %reduce-scatter.10.cloned.1.call-start = ((), (), s32[]{:S(2)}) async-start(), calls=%async_computation.15 | async-start | bytes 2654208 | tf_op jit(solution)/shard_map/reduce_scatter | solution.py:260
  246.2 149.8 %copy-start.14 = (f32[1024,32]{0,1:T(8,128)S(1)}, f32[1024,32]{0,1:T(8,128)}, u32[]{:S(2)}) copy-start(f32[1024,32]{0,1:T(8,128)} %copy-done.13) | copy-start | bytes 393220
  246.2 149.8 %copy-start.16 = (f32[1024,32]{0,1:T(8,128)S(1)}, f32[1024,32]{0,1:T(8,128)}, u32[]{:S(2)}) copy-start(f32[1024,32]{0,1:T(8,128)} %copy-done.15) | copy-start | bytes 393220
  401.1 1.3 copy-start.22
  401.1 1.3 copy-start.24
  401.2 1.1 copy-start.10
  405.3 74.2 %reduce-scatter.8.cloned.1.call-start = ((), (), s32[]{:S(2)}) async-start(), calls=%async_computation.14 | async-start | bytes 2654208 | tf_op jit(solution)/shard_map/reduce_scatter | solution.py:259
  406.8 1.1 copy-start.11
  410.9 106.9 %reduce-scatter.12.cloned.1.call-start = ((), (), s32[]{:S(2)}) async-start(), calls=%async_computation.16 | async-start | bytes 2654208 | tf_op jit(solution)/shard_map/reduce_scatter | solution.py:261
  413.9 174.7 %reduce-scatter.16.cloned.1.call-start = ((), (), s32[]{:S(2)}) async-start(), calls=%async_computation.18 | async-start | bytes 7077888 | tf_op jit(solution)/shard_map/reduce_scatter | solution.py:263
  422.7 236.5 %reduce-scatter.18.cloned.1.call-start = ((), (), s32[]{:S(2)}) async-start(), calls=%async_computation.19 | async-start | bytes 7077888 | tf_op jit(solution)/shard_map/reduce_scatter | solution.py:264
  431.7 297.8 %reduce-scatter.20.cloned.1.call-start = ((), (), s32[]{:S(2)}) async-start(), calls=%async_computation.20 | async-start | bytes 7077888 | tf_op jit(solution)/shard_map/reduce_scatter | solution.py:265
  440.7 356.7 %all-reduce.10.cloned.1.call-start = ((), (), s32[]{:S(2)}) async-start(), calls=%async_computation.21 | async-start | bytes 3538944 | tf_op jit(solution)/shard_map/psum | solution.py:270
  797.4 5.9 copy-start.20
  797.4 6.6 copy-start.19
  797.4 7.4 copy-start.18
  797.4 8.1 copy-start.17
Sparse Core Ops, SparseCore 0:
  9.6 30.6 all-gather.7
  42.0 28.8 all-gather.9
  72.6 21.2 all-gather.11
  95.4 37.8 all-gather.13
  134.8 37.1 all-gather.15
  173.4 37.1 all-gather.17
  212.2 21.6 all-gather.19
  246.3 35.9 reduce-scatter.13
  405.4 35.9 reduce-scatter.9
  443.5 35.9 reduce-scatter.7
  481.8 35.9 reduce-scatter.11
  519.9 68.6 reduce-scatter.15
  590.9 68.1 reduce-scatter.17
  661.3 68.1 reduce-scatter.19
  734.4 62.8 all-reduce.9
